TPU v7x, 32 devices: a whole 2x2x4 slice. The times are simulated.
32 devices in a mesh: section: 4 (over y, x), mp: 8 (over z, core).
Axes of the slice: x: 2, y: 2, z: 4, core: 2. Of those that a mesh axis runs over, the one named last changes fastest.
Arguments:
- stream: bfloat16 [512, 4096], P(('section', 'mp')), may hold values from -6 to 6
- ffn_gain: float32 [4096], replicated, may hold values from 0.25 to 1.75
- router_weight: bfloat16 [4096, 4], replicated, may hold values from -0.1875 to 0.1875
- expert_ids: int32 [512, 2], P(('section', 'mp')), may hold values from 0 to 3, all different within a row; in each aligned block of 16 rows (0 to 15, 16 to 31, ...) at most 12 rows name the same one
- w_gate: bfloat16 [4, 4096, 14336], P('section', None, 'mp'), may hold values from -0.09375 to 0.09375
- w_up: bfloat16 [4, 4096, 14336], P('section', None, 'mp'), may hold values from -0.09375 to 0.09375
- w_down: bfloat16 [4, 14336, 4096], P('section', 'mp'), may hold values from -0.09375 to 0.09375
- attn_gain: float32 [4096], replicated, may hold values from 0.25 to 1.75
- w_kv: bfloat16 [4096, 2048], P(None, 'mp'), may hold values from -0.09375 to 0.09375
Outputs:
- stream_out: bfloat16 [512, 4096], P(('section', 'mp'))
- kv_decode: bfloat16 [512, 2048], P('section', 'mp')
Inputs may be any that keep to these rules, and one draw needn't show every extreme that they name: `expert_ids`: each row names two different experts. Among the rows of one device no expert is named more than 12 times, a bound that some block reaches.
All inputs are finite; a program needn't handle non-finite values.
Results may differ from a plain program's by a relative error of at most 0.02.
Values may be sent and summed in bfloat16 or wider, within the bound.
A program may use at most 128 MiB of HBM per device.

v0:
```python
import jax
import jax.numpy as jnp
from jax import lax
from jax.sharding import PartitionSpec as P

epsilon = 1e-05


def shifted(value, axis, steps):
    count = lax.axis_size(axis)
    pairs = [(source, (source + steps) % count) for source in range(count)]
    return lax.ppermute(value, axis, pairs)


def normalize(values, scale_gain):
    floats = values.astype(jnp.float32)
    return (
        floats * lax.rsqrt(jnp.mean(floats * floats, axis=-1, keepdims=True) + epsilon) * scale_gain
    )


def body(stream, ffn_gain, router_weight, expert_ids, w_gate, w_up, w_down, attn_gain, w_kv):
    own_rows = stream.shape[0]
    model_width = stream.shape[1]
    experts = router_weight.shape[1]
    capacity = min(own_rows, 3 * own_rows // experts)
    normed = normalize(stream, ffn_gain).astype(jnp.bfloat16)
    logits = jnp.dot(normed, router_weight, preferred_element_type=jnp.float32)
    onehot = expert_ids[:, :, None] == jnp.arange(experts, dtype=jnp.int32)[None, None, :]
    chosen = jnp.sum(jnp.where(onehot, logits[:, None, :], jnp.float32(0.0)), axis=-1)
    share_first = jax.nn.sigmoid(chosen[:, 0] - chosen[:, 1])
    flat_hits = onehot.reshape(own_rows * 2, experts).astype(jnp.int32)
    before = jnp.cumsum(flat_hits, axis=0) - flat_hits
    slot_index = jnp.sum(before * flat_hits, axis=-1)
    expert_flat = expert_ids.reshape(-1)
    route_table = (
        expert_flat[None, None, :] == jnp.arange(experts, dtype=jnp.int32)[:, None, None]
    ) & (slot_index[None, None, :] == jnp.arange(capacity, dtype=jnp.int32)[None, :, None])
    route_table = route_table.astype(jnp.bfloat16)
    repeated = jnp.repeat(normed, 2, axis=0)
    buffer = jnp.einsum(
        "ecr,rd->ecd", route_table, repeated, preferred_element_type=jnp.float32
    ).astype(jnp.bfloat16)
    arrived = lax.all_to_all(buffer, "section", split_axis=0, concat_axis=0, tiled=True)
    inbound = arrived.reshape(experts * capacity, model_width)
    gate_weight = w_gate[0]
    up_weight = w_up[0]
    down_weight = w_down[0]
    block_rows = lax.all_gather(inbound, "mp", axis=0, tiled=True)
    gate_part = jnp.dot(block_rows, gate_weight, preferred_element_type=jnp.float32)
    up_part = jnp.dot(block_rows, up_weight, preferred_element_type=jnp.float32)
    hidden_all = (jax.nn.silu(gate_part) * up_part).astype(jnp.bfloat16)
    block_rows = hidden_all
    summed = lax.psum_scatter(
        jnp.dot(block_rows, down_weight, preferred_element_type=jnp.float32).astype(jnp.bfloat16),
        "mp",
        scatter_dimension=0,
        tiled=True,
    )
    results = summed.reshape(experts, capacity, model_width)
    returned = lax.all_to_all(results, "section", split_axis=0, concat_axis=0, tiled=True)
    picked = jnp.einsum("ecr,ecd->rd", route_table, returned, preferred_element_type=jnp.float32)
    picked = picked.reshape(own_rows, 2, model_width)
    updated = (
        stream.astype(jnp.float32)
        + share_first[:, None] * picked[:, 0]
        + (1.0 - share_first)[:, None] * picked[:, 1]
    )
    stream_out = updated.astype(jnp.bfloat16)
    attn_input = normalize(stream_out, attn_gain).astype(jnp.bfloat16)
    kv_local = jnp.dot(
        lax.all_gather(attn_input, "mp", axis=0, tiled=True),
        w_kv,
        preferred_element_type=jnp.float32,
    ).astype(jnp.bfloat16)
    kv_decode = shifted(kv_local, "section", 1)
    return (stream_out, kv_decode)


def solution(mesh):
    in_specs = (
        P(("section", "mp"), None),
        P(),
        P(),
        P(("section", "mp"), None),
        P("section", None, "mp"),
        P("section", None, "mp"),
        P("section", "mp", None),
        P(),
        P(None, "mp"),
    )
    out_specs = (P(("section", "mp"), None), P("section", "mp"))
    return jax.shard_map(body, mesh=mesh, in_specs=in_specs, out_specs=out_specs, check_vma=False)
```

profile of v0, /device:TPU:0, one launch (start us, length us, event | category | flops | bytes accessed | tf_op | source)
XLA Modules:
  0.0 191.3 jit_solution(9461943533034778147)
XLA Ops:
  7.2 0.9 copy.21
  8.3 1.1 fusion.21
  9.6 1.0 fusion.23
  10.9 0.3 convolution_convert_fusion
  11.2 13.5 %all_to_all.10 = bf16[4,12,4096]{2,1,0:T(8,128)(2,1)S(1)} all-to-all(bf16[4,12,4096]{2,1,0:T(8,128)(2,1)S(1)} %convolution_convert_fusion), channel_id=1, replica_groups=mesh['section'=4,'mp'=8] {'section'}, dimensions={0} | all-to-all | bytes 786432 | tf_op jit(solution)/shard_map/all_to_all | solution.py:44
  24.7 0.8 reshape.88
  25.7 38.0 %all-gather.3.cloned.1.call-done = bf16[384,4096]{1,0:T(8,128)(2,1)} async-done(((bf16[48,4096]{1,0:T(8,128)(2,1)}), bf16[384,4096]{1,0:T(8,128)(2,1)}) %all-gather.3.cloned.1.call-update) | async-done | bytes 3145744 | tf_op jit(solution)/shard_map/all_gather | solution.py:49
  63.7 12.9 %fusion.4 = f32[384,1792]{1,0:T(8,128)} fusion(bf16[384,4096]{1,0:T(8,128)(2,1)} %all-gather.3.cloned.1.call-done, bf16[1,4096,1792]{2,1,0:T(8,128)(2,1)} %param.13), kind=kOutput, calls=%fused_computation.4 | convolution fusion | flops 5637144576 | bytes 20578304 | tf_op jit(solution)/shard_map/dot_general | solution.py:50
  76.6 25.0 %fusion.6 = bf16[384,4096]{1,0:T(8,128)(2,1)} fusion(bf16[1,1792,4096]{2,1,0:T(8,128)(2,1)} %param.15, bf16[384,4096]{1,0:T(8,128)(2,1)} %all-gather.3.cloned.1.call-done, bf16[1,4096,1792]{2,1,0:T(8,128)(2,1)} %param.14, f32[384,1792]{1,0:T(8,128)} %fusion.4), kind=kOutput, calls=%fused_computation.6 | convolution fusion | flops 11279990784 | bytes 38404096 | tf_op jit(solution)/shard_map/dot_general | solution.py:55
  101.6 0.7 copy-done.5
  102.5 38.6 %reduce-scatter.2.cloned.1.call-done = bf16[48,4096]{1,0:T(8,128)(2,1)} async-done(((bf16[384,4096]{1,0:T(8,128)(2,1)}), bf16[48,4096]{1,0:T(8,128)(2,1)}) %reduce-scatter.2.cloned.1.call-update) | async-done | bytes 393232 | tf_op jit(solution)/shard_map/reduce_scatter | solution.py:54
  141.1 1.9 reshape.89
  143.0 3.7 %all-to-all-start.1 = ((bf16[4,12,4096]{2,1,0:T(8,128)(2,1)}), bf16[4,12,4096]{2,1,0:T(8,128)(2,1)S(1)}, u32[]{:S(2)}, u32[]{:S(2)}) async-start(bf16[4,12,4096]{2,1,0:T(8,128)(2,1)} %reshape.89), calls=%async_computation.2 | async-start | bytes 1048576 | tf_op jit(solution)/shard_map/all_to_all | solution.py:61
  146.7 6.5 %all-to-all-done.1 = bf16[4,12,4096]{2,1,0:T(8,128)(2,1)S(1)} async-done(((bf16[4,12,4096]{2,1,0:T(8,128)(2,1)}), bf16[4,12,4096]{2,1,0:T(8,128)(2,1)S(1)}, u32[]{:S(2)}, u32[]{:S(2)}) %all-to-all-start.1) | async-done | bytes 393248 | tf_op jit(solution)/shard_map/all_to_all | solution.py:61
  153.2 0.3 convolution_bitcast_fusion
  153.5 0.3 reshape.90
  153.8 0.5 fusion.37
  154.4 0.4 fusion.18
  154.8 0.7 fusion.20
  155.6 21.7 %all-gather.5.cloned.1.call-done = bf16[128,4096]{1,0:T(8,128)(2,1)} async-done(((bf16[16,4096]{1,0:T(8,128)(2,1)}), bf16[128,4096]{1,0:T(8,128)(2,1)}) %all-gather.5.cloned.1.call-update) | async-done | bytes 1048592 | tf_op jit(solution)/shard_map/all_gather | solution.py:72
  177.2 1.7 convolution_convert_fusion.1
  178.9 1.5 collective-permute-start
  180.4 3.7 %collective-permute-done = bf16[128,256]{1,0:T(8,128)(2,1)S(1)} collective-permute-done((bf16[128,256]{1,0:T(8,128)(2,1)S(1)}, bf16[128,256]{1,0:T(8,128)(2,1)S(1)}, u32[]{:S(2)}, u32[]{:S(2)}) %collective-permute-start) | collective-permute-done | bytes 65568 | tf_op jit(solution)/shard_map/ppermute | solution.py:12
  184.1 0.6 copy.39
  (30 shorter events, 1.1 us)
Async XLA Ops:
  7.2 170.1 %copy-start = (bf16[4096,256]{1,0:T(8,128)(2,1)S(1)}, bf16[4096,256]{1,0:T(8,128)(2,1)}, u32[]{:S(2)}) copy-start(bf16[4096,256]{1,0:T(8,128)(2,1)} %param.17) | copy-start | bytes 6291460
  7.2 56.5 %all-gather.3.cloned.1.call-start = ((), (), s32[]{:S(2)}) async-start(), calls=%async_computation.3 | async-start | bytes 3538944 | tf_op jit(solution)/shard_map/all_gather | solution.py:49
  25.6 115.5 %reduce-scatter.2.cloned.1.call-start = ((), (), s32[]{:S(2)}) async-start(), calls=%async_computation.4 | async-start | bytes 3538944 | tf_op jit(solution)/shard_map/reduce_scatter | solution.py:54
  101.6 0.8 copy-start.5
  101.6 45.0 %copy-start.4 = (s32[16,2]{0,1:T(2,128)S(1)}, s32[16,2]{0,1:T(2,128)}, u32[]{:S(2)}) copy-start(s32[16,2]{0,1:T(2,128)} %param.12) | copy-start | bytes 388
  102.4 52.0 %copy-start.1 = (bf16[16,4096]{1,0:T(8,128)(2,1)S(1)}, bf16[16,4096]{1,0:T(8,128)(2,1)}, u32[]{:S(2)}) copy-start(bf16[16,4096]{1,0:T(8,128)(2,1)} %param.9) | copy-start | bytes 393220
  102.4 52.4 %copy-start.3 = (f32[4096]{0:T(1024)S(1)}, f32[4096]{0:T(1024)}, u32[]{:S(2)}) copy-start(f32[4096]{0:T(1024)} %param.16) | copy-start | bytes 49156
  143.0 10.2 %all-to-all-start.1 = ((bf16[4,12,4096]{2,1,0:T(8,128)(2,1)}), bf16[4,12,4096]{2,1,0:T(8,128)(2,1)S(1)}, u32[]{:S(2)}, u32[]{:S(2)}) async-start(bf16[4,12,4096]{2,1,0:T(8,128)(2,1)} %reshape.89), calls=%async_computation.2 | async-start | bytes 1048576 | tf_op jit(solution)/shard_map/all_to_all | solution.py:61
  146.6 30.6 %all-gather.5.cloned.1.call-start = ((), (), s32[]{:S(2)}) async-start(), calls=%async_computation.5 | async-start | bytes 1179648 | tf_op jit(solution)/shard_map/all_gather | solution.py:72
  154.8 30.0 %copy-start.2 = (bf16[16,4096]{1,0:T(8,128)(2,1)}, bf16[16,4096]{1,0:T(8,128)(2,1)S(1)}, u32[]{:S(2)}) copy-start(bf16[16,4096]{1,0:T(8,128)(2,1)S(1)} %get-tuple-element.10) | copy-start | bytes 393220
  178.9 5.2 %collective-permute-start = (bf16[128,256]{1,0:T(8,128)(2,1)S(1)}, bf16[128,256]{1,0:T(8,128)(2,1)S(1)}, u32[]{:S(2)}, u32[]{:S(2)}) collective-permute-start(bf16[128,256]{1,0:T(8,128)(2,1)S(1)} %convolution_convert_fusion.1), channel_id=1, source_target_pairs={{0,8},{8,16},{16,24},{24,0},{1,9},{9,17},{17,25},{25,1},{2,10},{10... | collective-permute-start | bytes 196616 | tf_op jit(solution)/shard_map/ppermute | solution.py:12
Sparse Core Ops, SparseCore 0:
  25.7 37.9 all-gather.2
  101.8 39.2 reduce-scatter.1
  155.7 21.4 all-gather.4
where the time goes:
time: 192 us; the launch traced here: 191 us
  waiting for transfers between devices  109 us (57%)
  matrix products  40.3 us (21%)
  between operations  13.9 us (7%)
  blocking collectives  13.5 us (7%)
  local copies, waits for them, and re-layouts  6.24 us (3%)
  starting transfers between devices  5.26 us (3%)
  other arithmetic  3.58 us (2%)
    reduce_scatter x1, waiting for transfers between devices, body(): lax.psum_scatter(jnp.dot(block_rows, down_weight, preferred_element_type=...  38.6 us
    all_gather x1, waiting for transfers between devices, body(): block_rows = lax.all_gather(inbound, 'mp', axis=0, tiled=True)  38 us
    dot_general x1, matrix products, body(): jnp.dot(block_rows, down_weight, preferred_element_type=jnp.float32)  25 us
    all_gather x1, waiting for transfers between devices, body(): lax.all_gather(attn_input, 'mp', axis=0, tiled=True)  21.7 us
    all_to_all x1, blocking collectives, body(): lax.all_to_all(buffer, 'section', split_axis=0, concat_axis=0, tiled=True)  13.5 us
    dot_general x1, matrix products, body(): jnp.dot(block_rows, gate_weight, preferred_element_type=jnp.float32)  12.9 us
    all_to_all x1, waiting for transfers between devices, body(): lax.all_to_all(results, 'section', split_axis=0, concat_axis=0, tiled=True)  6.54 us
  transfers between devices with their start and end apart: 5, of which 5 were waited for; matrix products, arithmetic and copies ran while one was open for 0% of the time, Pallas kernels for 0%

commit v1 on v0

--- a/solution.py
+++ b/solution.py
@@ -1,6 +1,10 @@
+import functools
+
 import jax
 import jax.numpy as jnp
 from jax import lax
+from jax.experimental import pallas as pl
+from jax.experimental.pallas import tpu as pltpu
 from jax.sharding import PartitionSpec as P
 
 epsilon = 1e-05
@@ -19,7 +23,7 @@
     )
 
 
-def body(stream, ffn_gain, router_weight, expert_ids, w_gate, w_up, w_down, attn_gain, w_kv):
+def plain_body(stream, ffn_gain, router_weight, expert_ids, w_gate, w_up, w_down, attn_gain, w_kv):
     own_rows = stream.shape[0]
     model_width = stream.shape[1]
     experts = router_weight.shape[1]
@@ -77,6 +81,377 @@
     return (stream_out, kv_decode)
 
 
+MESH = pl.DeviceIdType.MESH
+f32, bf16 = jnp.float32, jnp.bfloat16
+SLOTS = 4
+VMEM_BYTES = 67043328
+LANES = 128
+
+
+def fused_kernel(
+    sections, layers, chunks,
+    stream, ffn_gain, router_t, ids, attn_gain, wg_hbm, wu_hbm, wd_hbm, wkv_hbm,
+    out, kv_out,
+    x_all, mix_all, wg, wu, wd, wkv, gate, up, hidden, part, pair_in, xd_in, yd_in, x_in, y_in, z_in,
+    attn, kv_mine, kv_in, weight,
+    g_send, g_recv, r_send, r_recv, w_sem, d_sem, k_send, k_recv,
+):
+    own, width = stream.shape
+    cc = width // chunks
+    rows = 2 * sections * layers * own
+    hid = hidden.shape[1]
+    tile = 256 if hid % 256 == 0 else LANES
+    s, m = lax.axis_index("section"), lax.axis_index("mp")
+    z, k = m // 2, m % 2
+    x, y = s % 2, s // 2
+    sx, sy, sd = y * 2 + (1 - x), (1 - y) * 2 + x, (1 - y) * 2 + (1 - x)
+    half = layers // 2
+    to_x, to_y = {"section": sx, "mp": m}, {"section": sy, "mp": m}
+    partner = {"section": s, "mp": z * 2 + 1 - k}
+
+    def z_peer(d):
+        return (z + d) % layers
+
+    def z_dev(d):
+        return {"section": s, "mp": z_peer(d) * 2 + k}
+
+    def load(c):
+        slot = c % SLOTS
+        at = pl.ds(c * cc, cc)
+        return (
+            pltpu.make_async_copy(wg_hbm.at[0, at], wg.at[slot], w_sem.at[slot, 0]),
+            pltpu.make_async_copy(wu_hbm.at[0, at], wu.at[slot], w_sem.at[slot, 1]),
+        )
+
+    def load_down():
+        return (
+            pltpu.make_async_copy(wd_hbm.at[0], wd, d_sem.at[0]),
+            pltpu.make_async_copy(wkv_hbm, wkv, d_sem.at[1]),
+        )
+
+    for c in range(min(SLOTS, chunks)):
+        for copy in load(c):
+            copy.start()
+
+    barrier = pltpu.get_barrier_semaphore()
+    greet = [z_dev(d) for d in range(1, layers)] + [partner]
+    greet += [{"section": (s + d) % sections, "mp": m} for d in range(1, sections)]
+    for dev in greet:
+        pl.semaphore_signal(barrier, inc=1, device_id=dev, device_id_type=MESH)
+
+    floats = stream[...].astype(f32)
+    normed = floats * lax.rsqrt(jnp.mean(floats * floats, axis=-1, keepdims=True) + epsilon)
+    normed = (normed * ffn_gain[...]).astype(bf16)
+    for c in range(chunks):
+        x_all[c, k, s, z] = normed[:, c * cc : (c + 1) * cc]
+    wide = normed.astype(f32)
+    lane = lax.broadcasted_iota(jnp.int32, (own, LANES), 1)
+    first, second = ids[:, 0:1], ids[:, 1:2]
+    la, lb = jnp.zeros((own, 1), f32), jnp.zeros((own, 1), f32)
+    for e in range(router_t.shape[0]):
+        logit = jnp.sum(wide * router_t[e : e + 1, :].astype(f32), axis=-1, keepdims=True)
+        la = la + jnp.where(first == e, logit, 0.0)
+        lb = lb + jnp.where(second == e, logit, 0.0)
+    share = jax.nn.sigmoid(la - lb)
+    mix = jnp.where(lane == first, share, 0.0) + jnp.where(lane == second, 1.0 - share, 0.0)
+    high = mix.astype(bf16)
+    mix_all[k, s, z, :, 0:LANES] = high
+    mix_all[k, s, z, :, LANES : 2 * LANES] = (mix - high.astype(f32)).astype(bf16)
+    pl.semaphore_wait(barrier, len(greet))
+
+    pieces = [x_all.at[0], mix_all] + [x_all.at[c] for c in range(1, chunks)]
+    chunk_of = [0, None] + list(range(1, chunks))
+    count = len(pieces)
+    sent = []
+
+    def remote(src, dst, ss, rs, dev):
+        return pltpu.make_async_remote_copy(
+            src_ref=src, dst_ref=dst, send_sem=ss, recv_sem=rs, device_id=dev, device_id_type=MESH
+        )
+
+    def go(copy):
+        copy.start()
+        sent.append(copy)
+
+    def gz(i, d):
+        ref = pieces[i].at[k, s, z]
+        return remote(ref, ref, g_send.at[i, d - 1], g_recv.at[i, d - 1], z_dev(d))
+
+    base = layers - 1
+
+    def gcopy(i, j, ref, dev):
+        return remote(ref, ref, g_send.at[i, base + j], g_recv.at[i, base + j], dev)
+
+    def gx(i):
+        return gcopy(i, 0, pieces[i].at[k, s], to_x)
+
+    def gy(i):
+        return gcopy(i, 1, pieces[i].at[k, s], to_y)
+
+    def gfy(i):
+        return gcopy(i, 2, pieces[i].at[k, sx, pl.ds(0, half)], to_y)
+
+    def gfx(i):
+        return gcopy(i, 3, pieces[i].at[k, sy, pl.ds(half, layers - half)], to_x)
+
+    def gp(i, j):
+        return gcopy(i, 4 + j, pieces[i].at[k, (s, sx, sy, sd)[j]], partner)
+
+    for i in range(count):
+        for d in range(1, layers):
+            go(gz(i, d))
+
+    def gather_steps(t):
+        if t < count:
+            for d in range(1, layers):
+                gz(t, d).wait_recv()
+            go(gx(t))
+            go(gy(t))
+            go(gp(t, 0))
+        if 0 <= t - 1 < count:
+            gx(t - 1).wait_recv()
+            go(gfy(t - 1))
+            go(gp(t - 1, 1))
+            gy(t - 1).wait_recv()
+            go(gfx(t - 1))
+            go(gp(t - 1, 2))
+        if 0 <= t - 2 < count:
+            gfy(t - 2).wait_recv()
+            gfx(t - 2).wait_recv()
+            go(gp(t - 2, 3))
+        if 0 <= t - 3 < count:
+            for j in range(4):
+                gp(t - 3, j).wait_recv()
+
+    def gate_up(c):
+        slot = c % SLOTS
+        for copy in load(c):
+            copy.wait()
+
+        def step(n, carry):
+            at = pl.ds(pl.multiple_of(n * tile, tile), tile)
+            tokens = x_all[c].reshape(rows, cc)
+            g = jnp.dot(tokens, wg[slot, :, at], preferred_element_type=f32)
+            u = jnp.dot(tokens, wu[slot, :, at], preferred_element_type=f32)
+            if c > 0:
+                g = g + gate[:, at]
+                u = u + up[:, at]
+            if c < chunks - 1:
+                gate[:, at] = g
+                up[:, at] = u
+            else:
+                hidden[:, at] = (g / (1.0 + jnp.exp(-g)) * u * weight[:, 0:1]).astype(bf16)
+            return carry
+
+        lax.fori_loop(0, hid // tile, step, 0)
+        if c + SLOTS < chunks:
+            for copy in load(c + SLOTS):
+                copy.start()
+
+    for t in range(count + 3):
+        gather_steps(t)
+        if t == 3:
+            for copy in load_down():
+                copy.start()
+        if t >= 3:
+            c = chunk_of[t - 3]
+            if c is None:
+                both = mix_all[...].reshape(rows, 2 * LANES).astype(f32)
+                both = both[:, 0:LANES] + both[:, LANES : 2 * LANES]
+                at_lane = lax.broadcasted_iota(jnp.int32, (rows, LANES), 1)
+                mine = jnp.sum(jnp.where(at_lane == s, both, 0.0), axis=-1, keepdims=True)
+                weight[...] = jnp.broadcast_to(mine, (rows, LANES))
+            else:
+                gate_up(c)
+
+    def rcopy(c, j, src, dst, dev):
+        return remote(src, dst, r_send.at[c, j], r_recv.at[c, j], dev)
+
+    def r_pair(c):
+        return rcopy(c, 0, part.at[c, 1 - k], pair_in.at[c], partner)
+
+    def r_xd(c):
+        return rcopy(c, 1, part.at[c, k, sd, pl.ds(0, half)], xd_in.at[c], to_x)
+
+    def r_yd(c):
+        return rcopy(c, 2, part.at[c, k, sd, pl.ds(half, layers - half)], yd_in.at[c], to_y)
+
+    def r_x(c):
+        return rcopy(c, 3, part.at[c, k, sx], x_in.at[c], to_x)
+
+    def r_y(c):
+        return rcopy(c, 4, part.at[c, k, sy], y_in.at[c], to_y)
+
+    def r_z(c, d):
+        return rcopy(c, 5 + d, part.at[c, k, s, z_peer(d)], z_in.at[c, d - 1], z_dev(d))
+
+    def a_z(c, d):
+        ref = attn.at[c, k, z]
+        return rcopy(c, 5 + base + d, ref, ref, z_dev(d))
+
+    def a_pair(c):
+        ref = attn.at[c, k]
+        return rcopy(c, 5, ref, ref, partner)
+
+    def down(c):
+        for n in range(cc // tile):
+            lo = c * cc + n * tile
+            r = jnp.dot(hidden[...], wd[:, lo : lo + tile], preferred_element_type=f32)
+            part[c, :, :, :, :, n * tile : (n + 1) * tile] = r.astype(bf16).reshape(
+                2, sections, layers, own, tile
+            )
+
+    def plus(a, b):
+        return (a.astype(f32) + b.astype(f32)).astype(bf16)
+
+    group = 2 * layers * own
+    state = {"kv": jnp.zeros((group, wkv.shape[1]), f32), "ss": jnp.zeros((group, 1), f32)}
+
+    for copy in load_down():
+        copy.wait()
+    for t in range(chunks + 6):
+        if 0 <= t - 5 < chunks:
+            for d in range(1, layers):
+                a_z(t - 5, d).wait_recv()
+            go(a_pair(t - 5))
+        if 0 <= t - 4 < chunks:
+            c = t - 4
+            cols = slice(c * cc, (c + 1) * cc)
+            total = part[c, k, s, z].astype(f32)
+            for d in range(1, layers):
+                r_z(c, d).wait_recv()
+                total = total + z_in[c, d - 1].astype(f32)
+            updated = (stream[:, cols].astype(f32) + total).astype(bf16)
+            attn[c, k, z] = updated
+            for d in range(1, layers):
+                go(a_z(c, d))
+            out[:, cols] = updated
+        if 0 <= t - 3 < chunks:
+            c = t - 3
+            r_x(c).wait_recv()
+            r_y(c).wait_recv()
+            add = part[c, k, s].astype(f32) + x_in[c].astype(f32) + y_in[c].astype(f32)
+            part[c, k, s] = add.astype(bf16)
+            for d in range(1, layers):
+                go(r_z(c, d))
+        if 0 <= t - 2 < chunks:
+            c = t - 2
+            r_xd(c).wait_recv()
+            part[c, k, sy, 0:half] = plus(part[c, k, sy, 0:half], xd_in[c])
+            go(r_y(c))
+            r_yd(c).wait_recv()
+            part[c, k, sx, half:layers] = plus(part[c, k, sx, half:layers], yd_in[c])
+            go(r_x(c))
+        if 0 <= t - 1 < chunks:
+            c = t - 1
+            r_pair(c).wait_recv()
+            part[c, k] = plus(part[c, k], pair_in[c])
+            go(r_xd(c))
+            go(r_yd(c))
+        if t < chunks:
+            down(t)
+            go(r_pair(t))
+        if 0 <= t - 5 < chunks:
+            c = t - 5
+            cols = slice(c * cc, (c + 1) * cc)
+            a_pair(c).wait_recv()
+            values = attn[c].reshape(group, cc).astype(f32)
+            state["ss"] = state["ss"] + jnp.sum(values * values, axis=-1, keepdims=True)
+            scaled = (values * attn_gain[:, cols]).astype(bf16)
+            state["kv"] = state["kv"] + jnp.dot(scaled, wkv[cols, :], preferred_element_type=f32)
+    keys = state["kv"] * lax.rsqrt(state["ss"] / width + epsilon)
+    keys = keys.astype(bf16).reshape(2, layers, own, wkv.shape[1])
+    for core in range(2):
+        for layer in range(layers):
+            at = (layer * 2 + core) * own
+            kv_mine[at : at + own, :] = keys[core, layer]
+    onward = remote(
+        kv_mine, kv_in, k_send.at[0], k_recv.at[0], {"section": (s + 1) % sections, "mp": m}
+    )
+    go(onward)
+    onward.wait_recv()
+    kv_out[...] = kv_in[...]
+    for copy in sent:
+        copy.wait_send()
+
+
+def fused_body(sections, mp, chunks, stream, ffn_gain, router_weight, expert_ids, w_gate, w_up, w_down, attn_gain, w_kv):
+    own, width = stream.shape
+    layers = mp // 2
+    cc = width // chunks
+    hid = w_gate.shape[2]
+    rows = sections * mp * own
+    kvc = w_kv.shape[1]
+    vmem = pl.BlockSpec(memory_space=pltpu.VMEM)
+    hbm = pl.BlockSpec(memory_space=pl.ANY)
+    dma = pltpu.SemaphoreType.DMA
+    gathers, returns = layers - 1 + 8, 5 + 2 * layers - 1
+    flops = 6 * rows * width * hid
+    return pl.pallas_call(
+        functools.partial(fused_kernel, sections, layers, chunks),
+        out_shape=(
+            jax.ShapeDtypeStruct((own, width), bf16),
+            jax.ShapeDtypeStruct((mp * own, kvc), bf16),
+        ),
+        in_specs=[vmem] * 5 + [hbm] * 4,
+        out_specs=(vmem, vmem),
+        scratch_shapes=[
+            pltpu.VMEM((chunks, 2, sections, layers, own, cc), bf16),
+            pltpu.VMEM((2, sections, layers, own, 2 * LANES), bf16),
+            pltpu.VMEM((SLOTS, cc, hid), bf16),
+            pltpu.VMEM((SLOTS, cc, hid), bf16),
+            pltpu.VMEM((hid, width), bf16),
+            pltpu.VMEM((width, kvc), bf16),
+            pltpu.VMEM((rows, hid), f32),
+            pltpu.VMEM((rows, hid), f32),
+            pltpu.VMEM((rows, hid), bf16),
+            pltpu.VMEM((chunks, 2, sections, layers, own, cc), bf16),
+            pltpu.VMEM((chunks, sections, layers, own, cc), bf16),
+            pltpu.VMEM((chunks, layers // 2, own, cc), bf16),
+            pltpu.VMEM((chunks, layers - layers // 2, own, cc), bf16),
+            pltpu.VMEM((chunks, layers, own, cc), bf16),
+            pltpu.VMEM((chunks, layers, own, cc), bf16),
+            pltpu.VMEM((chunks, layers - 1, own, cc), bf16),
+            pltpu.VMEM((chunks, 2, layers, own, cc), bf16),
+            pltpu.VMEM((mp * own, kvc), bf16),
+            pltpu.VMEM((mp * own, kvc), bf16),
+            pltpu.VMEM((rows, LANES), f32),
+            dma((chunks + 1, gathers)),
+            dma((chunks + 1, gathers)),
+            dma((chunks, returns)),
+            dma((chunks, returns)),
+            dma((SLOTS, 2)),
+            dma((2,)),
+            dma((1,)),
+            dma((1,)),
+        ],
+        compiler_params=pltpu.CompilerParams(
+            collective_id=0, has_side_effects=True, vmem_limit_bytes=VMEM_BYTES
+        ),
+        cost_estimate=pl.CostEstimate(
+            flops=flops, bytes_accessed=6 * width * hid, transcendentals=rows * hid
+        ),
+        name="expert_feed_forward",
+    )(
+        stream, ffn_gain[None, :], router_weight.T, expert_ids, attn_gain[None, :],
+        w_gate, w_up, w_down, w_kv,
+    )
+
+
+def body(sections, mp, *args):
+    stream, router_weight, w_gate = args[0], args[2], args[4]
+    own, width = stream.shape
+    rows, hid = sections * mp * own, w_gate.shape[2]
+    chunks = width // 512
+    held = rows * width * 7 + rows * hid * 10 + width * hid * 2 + SLOTS * 2048 * hid
+    fits = held < VMEM_BYTES - (6 << 20)
+    shaped = sections == 4 and mp % 4 == 0 and own % 16 == 0 and width % 512 == 0
+    shaped = shaped and hid % LANES == 0 and router_weight.shape[1] == sections
+    if fits and shaped:
+        return fused_body(sections, mp, chunks, *args)
+    return plain_body(*args)
+
+
 def solution(mesh):
     in_specs = (
         P(("section", "mp"), None),
@@ -90,4 +465,5 @@
         P(None, "mp"),
     )
     out_specs = (P(("section", "mp"), None), P("section", "mp"))
-    return jax.shard_map(body, mesh=mesh, in_specs=in_specs, out_specs=out_specs, check_vma=False)
+    return jax.shard_map(
+        functools.partial(body, mesh.shape["section"], mesh.shape["mp"]), mesh=mesh, in_specs=in_specs, out_specs=out_specs, check_vma=False)

time: 192 us -> 114 us (0.59)
  waiting for transfers between devices: 109 us -> 0 us
  Pallas kernels: 0 us -> 108 us
  matrix products: 40.3 us -> 0 us
  blocking collectives: 13.5 us -> 0 us
  between operations: 13.9 us -> 0.64 us
  starting transfers between devices: 5.26 us -> 0 us
  other arithmetic: 3.58 us -> 0 us
    pallas_call x0 -> x1, Pallas kernels: none -> 108 us  [fused_body(): pl.pallas_call(functools.partial(fused_kernel, sections, layers, chunks),...]
    all_gather x2 -> x0, waiting for transfers between devices: 59.7 us -> none  [the longest x1 38 us: body(): block_rows = lax.all_gather(inbound, 'mp', axis=0, tiled=True)]
    dot_general x6 -> x0, matrix products: 40.3 us -> none  [the longest x1 25 us: body(): jnp.dot(block_rows, down_weight, preferred_element_type=jnp.float32)]
    reduce_scatter x1 -> x0, waiting for transfers between devices: 38.6 us -> none  [body(): lax.psum_scatter(jnp.dot(block_rows, down_weight, preferred_element_type=...]
    all_to_all x1 -> x0, blocking collectives: 13.5 us -> none  [body(): lax.all_to_all(buffer, 'section', split_axis=0, concat_axis=0, tiled=True)]
    all_to_all x1 -> x0, waiting for transfers between devices: 6.54 us -> none  [body(): lax.all_to_all(results, 'section', split_axis=0, concat_axis=0, tiled=True)]
    ppermute x1 -> x0, waiting for transfers between devices: 3.7 us -> none  [shifted(): return lax.ppermute(value, axis, pairs)]
    all_to_all x1 -> x0, starting transfers between devices: 3.65 us -> none  [body(): lax.all_to_all(results, 'section', split_axis=0, concat_axis=0, tiled=True)]
  transfers between devices with their start and end apart: 5 -> 0, of which waited for: 5 -> 0; matrix products, arithmetic and copies ran while one was open for 0% -> 0% of each run, Pallas kernels for 0% -> 0%
where the time goes in v1:
time: 114 us; the launch traced here: 113 us
  Pallas kernels  108 us (95%)
  local copies, waits for them, and re-layouts  4.39 us (4%)
    pallas_call x1, Pallas kernels, fused_body(): pl.pallas_call(functools.partial(fused_kernel, sections, layers, chunks),...  108 us
    unnamed x3, local copies, waits for them, and re-layouts  4.39 us

profile of v1, /device:TPU:0, one launch (start us, length us, event | category | flops | bytes accessed | tf_op | source)
XLA Modules:
  0.0 113.5 jit_solution(5773343197291259466)
XLA Ops:
  0.6 1.4 %copy.11.ids = s32[16,2]{1,0:T(8,128)} copy(s32[16,2]{0,1:T(2,128)} %param.12) | data formatting | bytes 256 | tf_op args[3]
  2.0 108.5 %expert_feed_forward.1 = (bf16[16,4096]{1,0:T(8,128)(2,1)}, bf16[128,256]{1,0:T(8,128)(2,1)}) custom-call(bf16[16,4096]{1,0:T(8,128)(2,1)} %stream.1, f32[1,4096]{1,0:T(1,128)} %bitcast.4, bf16[4,4096]{1,0:T(4,128)(2,1)} %bitcast.3, s32[16,2]{1,0:T(8,128)} %copy.11.ids, f32[1,4096]{1,0:T(1,128)} %bitcast.5, bf16[1,4096,1792]{2,1,0:T(8,128)(2,1)} %wg_hbm.1, ...), custom_call_target="tpu_custom_call" | custom-call | flops 22548578304 | bytes 44040192 | tf_op jit(solution)/shard_map/expert_feed_forward/pallas_call | solution.py:390
  110.4 1.6 %copy.14 = bf16[16,4096]{1,0:T(8,128)(2,1)} copy(bf16[16,4096]{1,0:T(8,128)(2,1)} %get-tuple-element.4) | data formatting | bytes 262144
  112.0 1.5 %copy.15 = bf16[128,256]{1,0:T(8,128)(2,1)} copy(bf16[128,256]{1,0:T(8,128)(2,1)} %get-tuple-element.5) | data formatting | bytes 131072

commit v2 on v1

--- a/solution.py
+++ b/solution.py
@@ -84,6 +84,9 @@
 MESH = pl.DeviceIdType.MESH
 f32, bf16 = jnp.float32, jnp.bfloat16
 SLOTS = 4
+Z_AHEAD = 3
+GATHER_LAG = (2, 4, 5)
+RETURN_LAG = (1, 3, 5, 7, 9, 10)
 VMEM_BYTES = 67043328
 LANES = 128
 
@@ -197,7 +200,7 @@
     def gp(i, j):
         return gcopy(i, 4 + j, pieces[i].at[k, (s, sx, sy, sd)[j]], partner)
 
-    for i in range(count):
+    for i in range(min(Z_AHEAD, count)):
         for d in range(1, layers):
             go(gz(i, d))
 
@@ -205,23 +208,27 @@
         if t < count:
             for d in range(1, layers):
                 gz(t, d).wait_recv()
+            if t + Z_AHEAD < count:
+                for d in range(1, layers):
+                    go(gz(t + Z_AHEAD, d))
             go(gx(t))
             go(gy(t))
             go(gp(t, 0))
-        if 0 <= t - 1 < count:
-            gx(t - 1).wait_recv()
-            go(gfy(t - 1))
-            go(gp(t - 1, 1))
-            gy(t - 1).wait_recv()
-            go(gfx(t - 1))
-            go(gp(t - 1, 2))
-        if 0 <= t - 2 < count:
-            gfy(t - 2).wait_recv()
-            gfx(t - 2).wait_recv()
-            go(gp(t - 2, 3))
-        if 0 <= t - 3 < count:
+        b, f, p = (t - lag for lag in GATHER_LAG)
+        if 0 <= b < count:
+            gx(b).wait_recv()
+            go(gfy(b))
+            go(gp(b, 1))
+            gy(b).wait_recv()
+            go(gfx(b))
+            go(gp(b, 2))
+        if 0 <= f < count:
+            gfy(f).wait_recv()
+            gfx(f).wait_recv()
+            go(gp(f, 3))
+        if 0 <= p < count:
             for j in range(4):
-                gp(t - 3, j).wait_recv()
+                gp(p, j).wait_recv()
 
     def gate_up(c):
         slot = c % SLOTS
@@ -248,13 +255,14 @@
             for copy in load(c + SLOTS):
                 copy.start()
 
-    for t in range(count + 3):
+    last = GATHER_LAG[2]
+    for t in range(count + last):
         gather_steps(t)
-        if t == 3:
+        if t == last:
             for copy in load_down():
                 copy.start()
-        if t >= 3:
-            c = chunk_of[t - 3]
+        if t >= last:
+            c = chunk_of[t - last]
             if c is None:
                 both = mix_all[...].reshape(rows, 2 * LANES).astype(f32)
                 both = both[:, 0:LANES] + both[:, LANES : 2 * LANES]
@@ -309,13 +317,14 @@
 
     for copy in load_down():
         copy.wait()
-    for t in range(chunks + 6):
-        if 0 <= t - 5 < chunks:
+    for t in range(chunks + RETURN_LAG[5]):
+        l1, l2, l3, l4, l5, l6 = (t - lag for lag in RETURN_LAG)
+        if 0 <= l5 < chunks:
             for d in range(1, layers):
-                a_z(t - 5, d).wait_recv()
-            go(a_pair(t - 5))
-        if 0 <= t - 4 < chunks:
-            c = t - 4
+                a_z(l5, d).wait_recv()
+            go(a_pair(l5))
+        if 0 <= l4 < chunks:
+            c = l4
             cols = slice(c * cc, (c + 1) * cc)
             total = part[c, k, s, z].astype(f32)
             for d in range(1, layers):
@@ -326,24 +335,24 @@
             for d in range(1, layers):
                 go(a_z(c, d))
             out[:, cols] = updated
-        if 0 <= t - 3 < chunks:
-            c = t - 3
+        if 0 <= l3 < chunks:
+            c = l3
             r_x(c).wait_recv()
             r_y(c).wait_recv()
             add = part[c, k, s].astype(f32) + x_in[c].astype(f32) + y_in[c].astype(f32)
             part[c, k, s] = add.astype(bf16)
             for d in range(1, layers):
                 go(r_z(c, d))
-        if 0 <= t - 2 < chunks:
-            c = t - 2
+        if 0 <= l2 < chunks:
+            c = l2
             r_xd(c).wait_recv()
             part[c, k, sy, 0:half] = plus(part[c, k, sy, 0:half], xd_in[c])
             go(r_y(c))
             r_yd(c).wait_recv()
             part[c, k, sx, half:layers] = plus(part[c, k, sx, half:layers], yd_in[c])
             go(r_x(c))
-        if 0 <= t - 1 < chunks:
-            c = t - 1
+        if 0 <= l1 < chunks:
+            c = l1
             r_pair(c).wait_recv()
             part[c, k] = plus(part[c, k], pair_in[c])
             go(r_xd(c))
@@ -351,8 +360,8 @@
         if t < chunks:
             down(t)
             go(r_pair(t))
-        if 0 <= t - 5 < chunks:
-            c = t - 5
+        if 0 <= l6 < chunks:
+            c = l6
             cols = slice(c * cc, (c + 1) * cc)
             a_pair(c).wait_recv()
             values = attn[c].reshape(group, cc).astype(f32)

time: 114 us -> 99 us (0.87)
  Pallas kernels: 108 us -> 93.8 us
    pallas_call x1, Pallas kernels: 108 us -> 93.8 us  [fused_body(): pl.pallas_call(functools.partial(fused_kernel, sections, layers, chunks),...]
where the time goes in v2:
time: 99 us; the launch traced here: 98.8 us
  Pallas kernels  93.8 us (95%)
  local copies, waits for them, and re-layouts  4.39 us (4%)
    pallas_call x1, Pallas kernels, fused_body(): pl.pallas_call(functools.partial(fused_kernel, sections, layers, chunks),...  93.8 us
    unnamed x3, local copies, waits for them, and re-layouts  4.39 us

profile of v2, /device:TPU:0, one launch (start us, length us, event | category | flops | bytes accessed | tf_op | source)
XLA Modules:
  0.0 98.8 jit_solution(10391178895904116618)
XLA Ops:
  0.6 1.4 %copy.11.ids = s32[16,2]{1,0:T(8,128)} copy(s32[16,2]{0,1:T(2,128)} %param.12) | data formatting | bytes 256 | tf_op args[3]
  2.0 93.8 %expert_feed_forward.1 = (bf16[16,4096]{1,0:T(8,128)(2,1)}, bf16[128,256]{1,0:T(8,128)(2,1)}) custom-call(bf16[16,4096]{1,0:T(8,128)(2,1)} %stream.1, f32[1,4096]{1,0:T(1,128)} %bitcast.4, bf16[4,4096]{1,0:T(4,128)(2,1)} %bitcast.3, s32[16,2]{1,0:T(8,128)} %copy.11.ids, f32[1,4096]{1,0:T(1,128)} %bitcast.5, bf16[1,4096,1792]{2,1,0:T(8,128)(2,1)} %wg_hbm.1, ...), custom_call_target="tpu_custom_call" | custom-call | flops 22548578304 | bytes 44040192 | tf_op jit(solution)/shard_map/expert_feed_forward/pallas_call | solution.py:399
  95.8 1.6 %copy.14 = bf16[16,4096]{1,0:T(8,128)(2,1)} copy(bf16[16,4096]{1,0:T(8,128)(2,1)} %get-tuple-element.4) | data formatting | bytes 262144
  97.4 1.5 %copy.15 = bf16[128,256]{1,0:T(8,128)(2,1)} copy(bf16[128,256]{1,0:T(8,128)(2,1)} %get-tuple-element.5) | data formatting | bytes 131072
